TPU v7x, 32 devices: a whole 2x2x4 slice. The times are simulated.
32 devices in a mesh: row: 4 (over y, x), col: 8 (over z, core).
Axes of the slice: x: 2, y: 2, z: 4, core: 2. Of those that a mesh axis runs over, the one named last changes fastest.
Arguments:
- patches: bfloat16 [32, 128, 768], P('row', 'col'), may hold values from -6 to 6
- w_patch: bfloat16 [768, 6144], replicated, may hold values from -0.21875 to 0.21875
- patch_bias: bfloat16 [6144], replicated, may hold values from -5 to 5
- ln_gain: bfloat16 [6144], replicated, may hold values from 0.5 to 1.5
- w_qkv: bfloat16 [6144, 3, 48, 128], P(None, None, 'col'), may hold values from -1 to 1
- qk_gain: float32 [2, 48, 128], P(None, 'col'), may hold values from 0 to 6, as said below
- w_out: bfloat16 [48, 128, 6144], P('col', None, 'row'), may hold values from -0.078125 to 0.078125
Outputs:
- attn_branch: bfloat16 [4096, 6144], P(('row', 'col'))
Inputs may be any that keep to these rules, and one draw needn't show every extreme that they name: `qk_gain`: positive gains.
All inputs are finite; a program needn't handle non-finite values.
Results may differ from a plain program's by a relative error of at most 0.015.
Values may be sent and summed in bfloat16 or wider, within the bound.
No kernel may reach another device: no remote copies, remote signals or barrier semaphores. Data moves between devices by JAX's collectives and lax.ppermute only.
A program may use at most 320 MiB of HBM per device.

v0:
```python
import math

import jax
import jax.numpy as jnp
from jax import lax
from jax.sharding import PartitionSpec as P

NORM_EPS = 1e-06


def sincos_table(row_ids, col_ids, model_width):
    quarter = model_width // 4
    frequency = 1.0 / 10000.0 ** (jnp.arange(quarter, dtype=jnp.float32) / quarter)
    row_angle = row_ids.astype(jnp.float32)[:, None] * frequency[None, :]
    col_angle = col_ids.astype(jnp.float32)[:, None] * frequency[None, :]
    return jnp.concatenate(
        [jnp.sin(row_angle), jnp.cos(row_angle), jnp.sin(col_angle), jnp.cos(col_angle)], axis=1
    )


def layer_norm(values, gain_row):
    mean_val = jnp.mean(values, axis=-1, keepdims=True)
    centered = values - mean_val
    variance = jnp.mean(centered * centered, axis=-1, keepdims=True)
    return centered * lax.rsqrt(variance + NORM_EPS) * gain_row


def local(patches, w_patch, patch_bias, ln_gain, w_qkv, qk_gain, w_out):
    tile_rows, tile_cols, pixel_width = patches.shape
    model_width = w_patch.shape[1]
    heads_here = w_qkv.shape[2]
    head_size = w_qkv.shape[3]
    col_count = lax.axis_size("col")
    block_tokens = tile_rows * tile_cols * col_count
    row_anchor = lax.axis_index("row") * tile_rows
    qkv_matrix = w_qkv.reshape(model_width, 3 * heads_here * head_size)
    bias_row = patch_bias.astype(jnp.float32)[None, :]
    gain_row = ln_gain.astype(jnp.float32)
    pixels = lax.all_gather(patches, "col", axis=1, tiled=True)
    piece_cols = pixels.shape[1]
    local_rows = jnp.repeat(jnp.arange(tile_rows, dtype=jnp.int32), piece_cols)
    local_cols = jnp.tile(jnp.arange(piece_cols, dtype=jnp.int32), tile_rows)
    flat_pixels = pixels.reshape(tile_rows * piece_cols, pixel_width)
    embedded = jnp.dot(flat_pixels, w_patch, preferred_element_type=jnp.float32) + bias_row
    embedded = embedded + sincos_table(row_anchor + local_rows, local_cols, model_width)
    normed = layer_norm(embedded, gain_row).astype(jnp.bfloat16)
    normed_piece = normed.reshape(tile_rows, piece_cols, model_width)
    project_piece_cols = normed_piece.shape[1]
    flat_normed = normed_piece.reshape(tile_rows * project_piece_cols, model_width)
    projected = jnp.dot(flat_normed, qkv_matrix, preferred_element_type=jnp.float32)
    projected = projected.reshape(tile_rows, project_piece_cols, 3 * heads_here * head_size)
    projected = projected.reshape(block_tokens, 3, heads_here, head_size)
    queries = layer_norm(projected[:, 0], qk_gain[0]).astype(jnp.bfloat16)
    keys_here = layer_norm(projected[:, 1], qk_gain[1]).astype(jnp.bfloat16)
    values_here = projected[:, 2].astype(jnp.bfloat16)
    query_heads = queries.transpose(1, 0, 2)
    scale_factor = 1.0 / math.sqrt(head_size)
    start_state = (
        jnp.full((heads_here, block_tokens), -1e30, jnp.float32),
        jnp.zeros((heads_here, block_tokens), jnp.float32),
        jnp.zeros((heads_here, block_tokens, head_size), jnp.float32),
    )
    key_piece = lax.all_gather(keys_here, "row", axis=0, tiled=True)
    value_piece = lax.all_gather(values_here, "row", axis=0, tiled=True)
    piece_len = key_piece.shape[0]
    key_block = math.gcd(piece_len, 1024)
    block_count = piece_len // key_block
    key_blocks = key_piece.reshape(block_count, key_block, heads_here, head_size)
    value_blocks = value_piece.reshape(block_count, key_block, heads_here, head_size)

    def step_block(state, block_args):
        run_peak, run_total, run_acc = state
        block_keys, block_values = block_args
        scores = (
            jnp.einsum("hqd,khd->hqk", query_heads, block_keys, preferred_element_type=jnp.float32)
            * scale_factor
        )
        new_peak = jnp.maximum(run_peak, jnp.max(scores, axis=2))
        rescale = jnp.exp(run_peak - new_peak)
        exponent = jnp.exp(scores - new_peak[:, :, None])
        new_total = run_total * rescale + jnp.sum(exponent, axis=2)
        weighted = jnp.einsum(
            "hqk,khd->hqd",
            exponent.astype(jnp.bfloat16),
            block_values,
            preferred_element_type=jnp.float32,
        )
        new_acc = run_acc * rescale[:, :, None] + weighted
        return ((new_peak, new_total, new_acc), None)

    final_state, unused = lax.scan(step_block, start_state, (key_blocks, value_blocks))
    peak_all, total_all, acc_all = final_state
    context = (acc_all / total_all[:, :, None]).astype(jnp.bfloat16)
    context = context.transpose(1, 0, 2).reshape(block_tokens, heads_here * head_size)
    out_weight = lax.all_gather(w_out, "row", axis=2, tiled=True).reshape(
        heads_here * head_size, model_width
    )
    return lax.psum_scatter(
        jnp.dot(context, out_weight, preferred_element_type=jnp.float32).astype(jnp.bfloat16),
        "col",
        scatter_dimension=0,
        tiled=True,
    )


def solution(mesh):
    return jax.shard_map(
        local,
        mesh=mesh,
        in_specs=(
            P("row", "col", None),
            P(),
            P(),
            P(),
            P(None, None, "col", None),
            P(None, "col", None),
            P("col", None, "row"),
        ),
        out_specs=P(("row", "col"), None),
        check_vma=False,
    )
```

profile of v0, /device:TPU:0, one launch (start us, length us, event | category | flops | bytes accessed | tf_op | source)
XLA Modules:
  0.0 631.0 jit_solution(16349719539641851866)
XLA Ops:
  8.0 36.8 %copy.13 = bf16[6144,3,6,128]{0,3,2,1:T(8,128)(2,1)} copy(bf16[6144,3,6,128]{3,0,2,1:T(8,128)(2,1)} %param.13) | data formatting | bytes 56623104 | tf_op args[4]
  44.9 46.9 %multiply_sine_fusion.1 = (f32[1024,1536]{1,0:T(8,128)}, f32[1024,1536]{1,0:T(8,128)}, f32[1024,1536]{1,0:T(8,128)}, f32[1024,1536]{1,0:T(8,128)}) fusion(f32[1536]{0:T(1024)S(1)} %negate_power_fusion, f32[1024]{0:T(1024)S(1)} %get-tuple-element.118, f32[1024]{0:T(1024)S(1)} %get-tuple-element.117), kind=kLoop, calls=%fused_computation.35 | loop fusion | flops 3145728 | bytes 25180160 | tf_op jit(solution)/shard_map/sin | solution.py:17
  91.8 24.2 %fusion.29 = (f32[1024]{0:T(1024)S(1)}, f32[1024,6144]{1,0:T(8,128)}) fusion(f32[1024,1536]{1,0:T(8,128)} %get-tuple-element.111, f32[1024,1536]{1,0:T(8,128)} %get-tuple-element.112, f32[1024,1536]{1,0:T(8,128)} %get-tuple-element.108, f32[1024,1536]{1,0:T(8,128)} %get-tuple-element.107, f32[6144]{0:T(1024)S(1)} %convert_element_type.52, ...), kind=kOutput, calls=%fused_computation.60 | convolution fusion | flops 9701424128 | bytes 61370368 | tf_op jit(solution)/shard_map/dot_general | solution.py:44
  126.2 36.4 %fusion.19 = f32[1024,3,6,128]{0,3,2,1:T(8,128)S(1)} fusion(bf16[6144,3,6,128]{0,3,2,1:T(8,128)(2,1)} %copy.13, f32[1024,6144]{1,0:T(8,128)} %get-tuple-element.116, f32[6144]{0:T(1024)S(1)} %convert_element_type.57, f32[1024]{0:T(1024)S(1)} %add_rsqrt_fusion.2, f32[1024]{0:T(1024)S(1)} %broadcast_multiply_fusion.2), kind=kOutput, calls=%fused_computation.22 | convolution fusion | flops 29016195072 | bytes 62947328 | tf_op jit(solution)/shard_map/dot_general | solution.py:50
  173.3 67.7 %all-gather.8.cloned.1.call-done = bf16[4096,6,128]{0,2,1:T(8,128)(2,1)} async-done(((bf16[1024,6,128]{0,2,1:T(8,128)(2,1)}), bf16[4096,6,128]{0,2,1:T(8,128)(2,1)}) %all-gather.8.cloned.1.call-update) | async-done | bytes 6291472 | tf_op jit(solution)/shard_map/all_gather | solution.py:63
  241.0 11.3 %reshape.81 = bf16[4,1024,6,128]{1,0,3,2:T(4,128)(2,1)} reshape(bf16[4096,6,128]{0,2,1:T(8,128)(2,1)} %all-gather.8.cloned.1.call-done) | data formatting | bytes 12582912 | tf_op jit(solution)/shard_map/reshape | solution.py:68
  252.4 11.4 %copy.16 = bf16[4,1024,6,128]{3,1,2,0:T(8,128)(2,1)} copy(bf16[4,1024,6,128]{1,0,3,2:T(4,128)(2,1)} %reshape.81) | data formatting | bytes 12582912
  263.7 49.2 %all-gather.12.cloned.1.call-done = bf16[4096,1,6,128]{0,3,2,1:T(8,128)(2,1)} async-done(((bf16[1024,1,6,128]{0,3,2,1:T(8,128)(2,1)}), bf16[4096,1,6,128]{0,3,2,1:T(8,128)(2,1)}) %all-gather.12.cloned.1.call-update) | async-done | bytes 6291472 | tf_op jit(solution)/shard_map/all_gather | solution.py:64
  313.0 11.4 %reshape.82 = bf16[4,1024,6,128]{1,0,3,2:T(4,128)(2,1)} reshape(bf16[4096,1,6,128]{0,3,2,1:T(8,128)(2,1)} %all-gather.12.cloned.1.call-done) | data formatting | bytes 12582912 | tf_op jit(solution)/shard_map/reshape | solution.py:69
  324.4 11.3 %copy.18 = bf16[4,1024,6,128]{3,1,2,0:T(8,128)(2,1)} copy(bf16[4,1024,6,128]{1,0,3,2:T(4,128)(2,1)} %reshape.82) | data formatting | bytes 12582912
  335.7 143.7 %while.15 = (s32[]{:T(128)}, f32[6,1024]{1,0:T(8,128)S(1)}, f32[6,1024]{1,0:T(8,128)S(1)}, f32[6,1024,128]{2,1,0:T(8,128)}, bf16[4,1024,6,128]{3,1,2,0:T(8,128)(...) while((s32[]{:T(128)}, f32[6,1024]{1,0:T(8,128)S(1)}, ...), condition=%wide.region_9.10_spmd.clone, body=%wide.region_6.9_spmd.clone.sunk | while | flops 3273947136 | bytes 86901856 | solution.py:91
  335.7 11.5 %bitcast_reduce_fusion.2 = (f32[6,1024]{1,0:T(8,128)S(1)}, f32[6,1024,1024]{2,1,0:T(8,128)}) fusion(bf16[6,1024,128]{2,1,0:T(8,128)(2,1)S(1)} %get-tuple-element.195, bf16[4,1024,6,128]{3,1,2,0:T(8,128)(2,1)} %get-tuple-element.194, s32[]{:T(128)} %get-tuple-element.181), kind=kOutput, calls=%fused_computation.1.clone.1 | convolution fusion | flops 1623189504 | bytes 28336640 | tf_op jit(solution)/shard_map/while/body/eval_jaxpr/hqd,khd->hqk/dot_general | solution.py:75
  357.7 14.2 %fusion.45 = f32[6,1024,128]{2,1,0:T(8,128)} fusion(f32[6,1024,128]{2,1,0:T(8,128)} %get-tuple-element.184, f32[6,1024,1024]{2,1,0:T(8,128)} %get-tuple-element.169, f32[6,1024]{1,0:T(8,128)S(1)} %select_maximum_fusion.2, bf16[4,1024,6,128]{3,1,2,0:T(8,128)(2,1)} %get-tuple-element.196, s32[]{:T(128)} %get-tuple-element.181, ...), kind=kOutput, calls=%fused_computation.9.clone.1 | convolution fusion | flops 1631846400 | bytes 33079808 | tf_op jit(solution)/shard_map/while/body/eval_jaxpr/hqk,khd->hqd/dot_general | solution.py:82
  371.9 11.5 %bitcast_reduce_fusion.2 = (f32[6,1024]{1,0:T(8,128)S(1)}, f32[6,1024,1024]{2,1,0:T(8,128)}) fusion(bf16[6,1024,128]{2,1,0:T(8,128)(2,1)S(1)} %get-tuple-element.195, bf16[4,1024,6,128]{3,1,2,0:T(8,128)(2,1)} %get-tuple-element.194, s32[]{:T(128)} %get-tuple-element.181), kind=kOutput, calls=%fused_computation.1.clone.1 | convolution fusion | flops 1623189504 | bytes 28336640 | tf_op jit(solution)/shard_map/while/body/eval_jaxpr/hqd,khd->hqk/dot_general | solution.py:75
  383.4 10.5 %fusion.43 = f32[6,1024]{1,0:T(8,128)S(1)} fusion(f32[6,1024,1024]{2,1,0:T(8,128)} %get-tuple-element.169, f32[6,1024]{1,0:T(8,128)S(1)} %select_maximum_fusion.2), kind=kLoop, calls=%fused_computation.4.clone.1 | loop fusion | flops 18868224 | bytes 25214976 | tf_op jit(solution)/shard_map/while/body/eval_jaxpr/reduce_sum | solution.py:81
  394.0 13.7 %fusion.45 = f32[6,1024,128]{2,1,0:T(8,128)} fusion(f32[6,1024,128]{2,1,0:T(8,128)} %get-tuple-element.184, f32[6,1024,1024]{2,1,0:T(8,128)} %get-tuple-element.169, f32[6,1024]{1,0:T(8,128)S(1)} %select_maximum_fusion.2, bf16[4,1024,6,128]{3,1,2,0:T(8,128)(2,1)} %get-tuple-element.196, s32[]{:T(128)} %get-tuple-element.181, ...), kind=kOutput, calls=%fused_computation.9.clone.1 | convolution fusion | flops 1631846400 | bytes 33079808 | tf_op jit(solution)/shard_map/while/body/eval_jaxpr/hqk,khd->hqd/dot_general | solution.py:82
  407.8 11.5 %bitcast_reduce_fusion.2 = (f32[6,1024]{1,0:T(8,128)S(1)}, f32[6,1024,1024]{2,1,0:T(8,128)}) fusion(bf16[6,1024,128]{2,1,0:T(8,128)(2,1)S(1)} %get-tuple-element.195, bf16[4,1024,6,128]{3,1,2,0:T(8,128)(2,1)} %get-tuple-element.194, s32[]{:T(128)} %get-tuple-element.181), kind=kOutput, calls=%fused_computation.1.clone.1 | convolution fusion | flops 1623189504 | bytes 28336640 | tf_op jit(solution)/shard_map/while/body/eval_jaxpr/hqd,khd->hqk/dot_general | solution.py:75
  419.2 10.5 %fusion.43 = f32[6,1024]{1,0:T(8,128)S(1)} fusion(f32[6,1024,1024]{2,1,0:T(8,128)} %get-tuple-element.169, f32[6,1024]{1,0:T(8,128)S(1)} %select_maximum_fusion.2), kind=kLoop, calls=%fused_computation.4.clone.1 | loop fusion | flops 18868224 | bytes 25214976 | tf_op jit(solution)/shard_map/while/body/eval_jaxpr/reduce_sum | solution.py:81
  429.8 13.7 %fusion.45 = f32[6,1024,128]{2,1,0:T(8,128)} fusion(f32[6,1024,128]{2,1,0:T(8,128)} %get-tuple-element.184, f32[6,1024,1024]{2,1,0:T(8,128)} %get-tuple-element.169, f32[6,1024]{1,0:T(8,128)S(1)} %select_maximum_fusion.2, bf16[4,1024,6,128]{3,1,2,0:T(8,128)(2,1)} %get-tuple-element.196, s32[]{:T(128)} %get-tuple-element.181, ...), kind=kOutput, calls=%fused_computation.9.clone.1 | convolution fusion | flops 1631846400 | bytes 33079808 | tf_op jit(solution)/shard_map/while/body/eval_jaxpr/hqk,khd->hqd/dot_general | solution.py:82
  443.6 11.5 %bitcast_reduce_fusion.2 = (f32[6,1024]{1,0:T(8,128)S(1)}, f32[6,1024,1024]{2,1,0:T(8,128)}) fusion(bf16[6,1024,128]{2,1,0:T(8,128)(2,1)S(1)} %get-tuple-element.195, bf16[4,1024,6,128]{3,1,2,0:T(8,128)(2,1)} %get-tuple-element.194, s32[]{:T(128)} %get-tuple-element.181), kind=kOutput, calls=%fused_computation.1.clone.1 | convolution fusion | flops 1623189504 | bytes 28336640 | tf_op jit(solution)/shard_map/while/body/eval_jaxpr/hqd,khd->hqk/dot_general | solution.py:75
  455.1 10.5 %fusion.43 = f32[6,1024]{1,0:T(8,128)S(1)} fusion(f32[6,1024,1024]{2,1,0:T(8,128)} %get-tuple-element.169, f32[6,1024]{1,0:T(8,128)S(1)} %select_maximum_fusion.2), kind=kLoop, calls=%fused_computation.4.clone.1 | loop fusion | flops 18868224 | bytes 25214976 | tf_op jit(solution)/shard_map/while/body/eval_jaxpr/reduce_sum | solution.py:81
  465.6 13.7 %fusion.45 = f32[6,1024,128]{2,1,0:T(8,128)} fusion(f32[6,1024,128]{2,1,0:T(8,128)} %get-tuple-element.184, f32[6,1024,1024]{2,1,0:T(8,128)} %get-tuple-element.169, f32[6,1024]{1,0:T(8,128)S(1)} %select_maximum_fusion.2, bf16[4,1024,6,128]{3,1,2,0:T(8,128)(2,1)} %get-tuple-element.196, s32[]{:T(128)} %get-tuple-element.181, ...), kind=kOutput, calls=%fused_computation.9.clone.1 | convolution fusion | flops 1631846400 | bytes 33079808 | tf_op jit(solution)/shard_map/while/body/eval_jaxpr/hqk,khd->hqd/dot_general | solution.py:82
  479.4 15.5 %bitcast_convert_fusion = bf16[1024,6144]{1,0:T(8,128)(2,1)} fusion(bf16[6,128,6144]{2,1,0:T(8,128)(2,1)} %all-gather.10.cloned.1.call-done, f32[6,1024,128]{2,1,0:T(8,128)} %get-tuple-element.43, f32[6,1024]{1,0:T(8,128)S(1)} %get-tuple-element.44), kind=kOutput, calls=%fused_computation.25 | convolution fusion | flops 9671540736 | bytes 25190400 | tf_op jit(solution)/shard_map/dot_general | solution.py:99
  494.9 129.6 %reduce-scatter.2.cloned.1.call-done = bf16[128,6144]{1,0:T(8,128)(2,1)} async-done(((bf16[1024,6144]{1,0:T(8,128)(2,1)}), bf16[128,6144]{1,0:T(8,128)(2,1)}) %reduce-scatter.2.cloned.1.call-update) | async-done | bytes 1572880 | tf_op jit(solution)/shard_map/reduce_scatter | solution.py:98
  (52 shorter events, 33.0 us)
Async XLA Ops:
  6.5 85.3 %all-gather.6.cloned.1.call-start = ((), (), s32[]{:S(2)}) async-start(), calls=%async_computation.1 | async-start | bytes 1769472 | tf_op jit(solution)/shard_map/all_gather | solution.py:39
  7.3 233.8 %all-gather.8.cloned.1.call-start = ((), (), s32[]{:S(2)}) async-start(), calls=%async_computation.2 | async-start | bytes 7864320 | tf_op jit(solution)/shard_map/all_gather | solution.py:63
  8.0 36.8 %copy-start.1 = (bf16[6144]{0:T(1024)(128)(2,1)S(1)}, bf16[6144]{0:T(1024)(128)(2,1)}, u32[]{:S(2)}) copy-start(bf16[6144]{0:T(1024)(128)(2,1)} %param.12) | copy-start | bytes 36868
  8.0 36.8 %copy-start.2 = (f32[2,6,128]{2,0,1:T(2,128)S(1)}, f32[2,6,128]{2,0,1:T(2,128)}, u32[]{:S(2)}) copy-start(f32[2,6,128]{2,0,1:T(2,128)} %param.14) | copy-start | bytes 18436
  162.7 3.6 copy-start
  168.1 144.8 %all-gather.12.cloned.1.call-start = ((), (), s32[]{:S(2)}) async-start(), calls=%async_computation.5 | async-start | bytes 7864320 | tf_op jit(solution)/shard_map/all_gather | solution.py:64
  171.5 307.9 %all-gather.10.cloned.1.call-start = ((), (), s32[]{:S(2)}) async-start(), calls=%async_computation.3 | async-start | bytes 11796480 | tf_op jit(solution)/shard_map/all_gather | solution.py:95
  172.1 452.4 %reduce-scatter.2.cloned.1.call-start = ((), (), s32[]{:S(2)}) async-start(), calls=%async_computation.4 | async-start | bytes 14155776 | tf_op jit(solution)/shard_map/reduce_scatter | solution.py:98
Sparse Core Ops, SparseCore 0:
  8.9 27.9 all-gather.5
  168.2 72.7 all-gather.7
  242.9 70.0 all-gather.11
  314.7 96.2 all-gather.9
  495.0 129.3 reduce-scatter.1
where the time goes:
time: 634 us; the launch traced here: 631 us
  waiting for transfers between devices  248 us (39%)
  matrix products  177 us (28%)
  other arithmetic  104 us (16%)
  local copies, waits for them, and re-layouts  88.6 us (14%)
  between operations  13.3 us (2%)
    reduce_scatter x1, waiting for transfers between devices, local(): lax.psum_scatter(jnp.dot(context, out_weight, preferred_element_type=jnp....  130 us
    all_gather x1, waiting for transfers between devices, local(): key_piece = lax.all_gather(keys_here, 'row', axis=0, tiled=True)  67.7 us
    unnamed x10, local copies, waits for them, and re-layouts  62.5 us
    dot_general x4, matrix products, step_block(): jnp.einsum('hqk,khd->hqd', exponent.astype(jnp.bfloat16), block_values, p...  55.5 us
    all_gather x1, waiting for transfers between devices, local(): value_piece = lax.all_gather(values_here, 'row', axis=0, tiled=True)  49.2 us
    sin x1, other arithmetic, sincos_table(): jnp.sin(row_angle)  46.9 us
    dot_general x4, matrix products, step_block(): jnp.einsum('hqd,khd->hqk', query_heads, block_keys, preferred_element_typ...  45.9 us
    reduce_sum x4, other arithmetic, step_block(): new_total = run_total * rescale + jnp.sum(exponent, axis=2)  42.2 us
  transfers between devices with their start and end apart: 5, of which 3 were waited for; matrix products, arithmetic and copies ran while one was open for 44% of the time, Pallas kernels for 0%

commit v1 on v0

v1 whole, which is shorter than its diff:
```python
import functools
import math

import jax
import jax.numpy as jnp
from jax import lax
from jax.experimental import pallas as pl
from jax.experimental.pallas import tpu as pltpu
from jax.sharding import Mesh, PartitionSpec as P

NORM_EPS = 1e-06
MIB = 1024 * 1024
NT = (((1,), (1,)), ((), ()))


def sincos_halves(ids, model_width):
    quarter = model_width // 4
    frequency = 1.0 / 10000.0 ** (jnp.arange(quarter, dtype=jnp.float32) / quarter)
    angle = ids.astype(jnp.float32)[:, None] * frequency[None, :]
    return jnp.concatenate([jnp.sin(angle), jnp.cos(angle)], axis=1)


def params(limit_mib, sem):
    return pltpu.CompilerParams(dimension_semantics=sem, vmem_limit_bytes=limit_mib * MIB)


def embed_body(px_ref, w_ref, bias_ref, gain_ref, row_ref, col_ref, out_ref, e_ref):
    rows, width, pixel = px_ref.shape
    tokens = rows * width
    model = w_ref.shape[1]
    half = model // 2
    px = px_ref[...].reshape(tokens, pixel)
    step = math.gcd(half, 1024)
    for n in range(0, model, step):
        part = jnp.dot(px, w_ref[:, n : n + step], preferred_element_type=jnp.float32)
        part = (part + bias_ref[:, n : n + step]).reshape(rows, width, step)
        if n < half:
            part = part + row_ref[:, :, n : n + step]
        else:
            part = part + col_ref[:, n - half : n - half + step][None]
        e_ref[:, n : n + step] = part.reshape(tokens, step)
    group = 16
    lanes = math.gcd(group * 4, tokens) // group

    def body(i, carry):
        for u in range(lanes):
            at = pl.ds(pl.multiple_of((i * lanes + u) * group, group), group)
            v = e_ref[at, :]
            mean = jnp.sum(v, axis=1, keepdims=True) * (1.0 / model)
            v = v - mean
            var = jnp.sum(v * v, axis=1, keepdims=True) * (1.0 / model)
            out_ref[at, :] = (v * lax.rsqrt(var + NORM_EPS) * gain_ref[...]).astype(out_ref.dtype)
        return carry

    lax.fori_loop(0, tokens // (group * lanes), body, 0)


def embed_norm(pixels, w_patch, bias_row, gain_row, row_table, col_table):
    rows, width, pixel = pixels.shape
    model = w_patch.shape[1]
    block = math.gcd(rows, max(1, 256 // width))
    once = pl.Buffered(1)
    return pl.pallas_call(
        embed_body,
        grid=(rows // block,),
        in_specs=[
            pl.BlockSpec((block, width, pixel), lambda i: (i, 0, 0)),
            pl.BlockSpec((pixel, model), lambda i: (0, 0), pipeline_mode=once),
            pl.BlockSpec((1, model), lambda i: (0, 0)),
            pl.BlockSpec((1, model), lambda i: (0, 0)),
            pl.BlockSpec((block, 1, model // 2), lambda i: (i, 0, 0)),
            pl.BlockSpec((width, model // 2), lambda i: (0, 0), pipeline_mode=once),
        ],
        out_specs=pl.BlockSpec((block * width, model), lambda i: (i, 0)),
        out_shape=jax.ShapeDtypeStruct((rows * width, model), jnp.bfloat16),
        scratch_shapes=[pltpu.VMEM((block * width, model), jnp.float32)],
        compiler_params=params(40, ("arbitrary",)),
        name="embed_norm",
    )(pixels, w_patch, bias_row, gain_row, row_table[:, None, :], col_table)


def project_body(x_ref, w_ref, *refs, norm, tile):
    gain_ref, out_ref = refs if norm else (None, refs[0])
    group, _, size = w_ref.shape
    w = jnp.concatenate([w_ref[h] for h in range(group)], axis=1)

    def body(i, carry):
        at = pl.ds(pl.multiple_of(i * tile, tile), tile)
        full = jnp.dot(x_ref[at, :], w, preferred_element_type=jnp.float32)
        for h in range(group):
            v = full[:, h * size : (h + 1) * size]
            if norm:
                v = v - jnp.mean(v, axis=1, keepdims=True)
                var = jnp.mean(v * v, axis=1, keepdims=True)
                v = v * lax.rsqrt(var + NORM_EPS) * gain_ref[h]
            out_ref[h, at, :] = v.astype(out_ref.dtype)
        return carry

    lax.fori_loop(0, x_ref.shape[0] // tile, body, 0)


def project(normed, weight, which, gain, name):
    tokens, model = normed.shape
    _, heads, _, size = weight.shape
    group = 2 if heads % 2 == 0 else heads
    norm = gain is not None
    in_specs = [
        pl.BlockSpec((tokens, model), lambda g: (0, 0), pipeline_mode=pl.Buffered(1)),
        pl.BlockSpec((None, group, model, size), lambda g: (which, g, 0, 0)),
    ]
    operands = [normed, weight]
    if norm:
        in_specs.append(pl.BlockSpec((group, 1, size), lambda g: (g, 0, 0)))
        operands.append(gain[:, None, :])
    return pl.pallas_call(
        functools.partial(project_body, norm=norm, tile=math.gcd(tokens, 512)),
        grid=(heads // group,),
        in_specs=in_specs,
        out_specs=pl.BlockSpec((group, tokens, size), lambda g: (g, 0, 0)),
        out_shape=jax.ShapeDtypeStruct((heads, tokens, size), jnp.bfloat16),
        compiler_params=params(40, ("arbitrary",)),
        name=name,
    )(*operands)


def attend_body(*refs, pairs, first, last, scale, key_block):
    q_ref, refs = refs[0], refs[1:]
    kv, refs = refs[: 2 * pairs], refs[2 * pairs :]
    if not first:
        peak_in, acc_in, refs = refs[0], refs[1], refs[2:]
    size = q_ref.shape[-1]
    rows = math.prod(q_ref.shape[:-1])
    q = q_ref[...].reshape(rows, size)
    ones = jnp.ones((key_block, size), jnp.bfloat16)
    blocks = []
    for c in range(pairs):
        for b in range(kv[2 * c].shape[0] // key_block):
            blocks.append((kv[2 * c], kv[2 * c + 1], b * key_block))

    def score(i):
        k_ref, _, at = blocks[i]
        return lax.dot_general(q, k_ref[at : at + key_block, :], NT, preferred_element_type=jnp.float32)

    if first:
        peak = None
        acc = None
    else:
        peak = peak_in[...].reshape(rows, size)[:, :1]
        acc = acc_in[...].reshape(rows, 2 * size)
    ahead = score(0)
    for i in range(len(blocks)):
        scores = ahead
        if i + 1 < len(blocks):
            ahead = score(i + 1)
        top = jnp.max(scores, axis=1, keepdims=True)
        new_peak = top if peak is None else jnp.maximum(peak, top)
        weights = jnp.exp2((scores - new_peak) * scale).astype(jnp.bfloat16)
        _, v_ref, at = blocks[i]
        v = jnp.concatenate([v_ref[at : at + key_block, :], ones], axis=1)
        mixed = jnp.dot(weights, v, preferred_element_type=jnp.float32)
        if peak is None:
            acc = mixed
        else:
            acc = acc * jnp.exp2((peak - new_peak) * scale) + mixed
        peak = new_peak
    if last:
        out_ref = refs[0]
        out_ref[...] = (acc[:, :size] / acc[:, size:]).astype(out_ref.dtype).reshape(out_ref.shape)
    else:
        refs[0][...] = jnp.broadcast_to(peak, (rows, size)).reshape(refs[0].shape)
        refs[1][...] = acc.reshape(refs[1].shape)


def attend(queries, kvs, state, pieces, part, parts, last, name):
    heads, tokens, size = queries.shape
    scale = math.log2(math.e) / math.sqrt(size)
    keys = kvs[0][0].shape[1]
    key_block = math.gcd(keys, 1024)
    run = tokens // pieces
    cut = run // parts
    if part is None:
        qb = math.gcd(tokens, 512)
        grid = (heads, tokens // qb)
        view = lambda a: a
        block = lambda width: pl.BlockSpec((None, qb, width), lambda h, i: (h, i, 0))
        out_rows = tokens
    else:
        grid = (heads, 1)
        qb = pieces * cut
        view = lambda a: a.reshape(heads, pieces, parts, cut, a.shape[-1])
        block = lambda width: pl.BlockSpec((None, pieces, None, cut, width), lambda h, i: (h, 0, part, 0, 0))
        out_rows = pieces * cut
    whole = pl.BlockSpec((None, keys, size), lambda h, i: (h, 0, 0))
    operands = [view(queries)]
    in_specs = [block(size)]
    for k, v in kvs:
        operands += [k, v]
        in_specs += [whole, whole]
    if state is not None:
        operands += [view(state[0]), view(state[1])]
        in_specs += [block(size), block(2 * size)]
    if last:
        out_specs = pl.BlockSpec((qb, size), lambda h, i: (i, h))
        out_shape = jax.ShapeDtypeStruct((out_rows, heads * size), jnp.bfloat16)
    else:
        out_specs = [block(size), block(2 * size)]
        out_shape = [
            jax.ShapeDtypeStruct((heads, tokens, size), jnp.float32),
            jax.ShapeDtypeStruct((heads, tokens, 2 * size), jnp.float32),
        ]
    return pl.pallas_call(
        functools.partial(
            attend_body, pairs=len(kvs), first=state is None, last=last, scale=scale, key_block=key_block
        ),
        grid=grid,
        in_specs=in_specs,
        out_specs=out_specs,
        out_shape=out_shape,
        compiler_params=params(40, ("arbitrary", "arbitrary")),
        name=name,
    )(*operands)


def swap(n, shift):
    return [(i, (i + shift) % n) for i in range(n)]


def local(patches, w_patch, patch_bias, ln_gain, w_qkv, qk_gain, w_out):
    tile_rows, tile_cols, pixel_width = patches.shape
    model = w_patch.shape[1]
    heads, size = w_qkv.shape[2], w_qkv.shape[3]
    ny, nx, nz, nc = (lax.axis_size(a) for a in ("y", "x", "z", "c"))
    row = lax.axis_index("y") * nx + lax.axis_index("x")
    z_at, c_at = lax.axis_index("z"), lax.axis_index("c")
    width = tile_cols * nz * nc

    out_weight = lax.all_gather(w_out, ("y", "x"), axis=2, tiled=True).reshape(heads * size, model)

    pieces = [patches] + [lax.ppermute(patches, "z", swap(nz, s)) for s in range(1, nz)]
    mine = jnp.stack(pieces)
    both = jnp.stack([mine, lax.ppermute(mine, "c", swap(nc, 1))])
    order_z = (z_at - jnp.arange(nz)) % nz
    order_c = (c_at - jnp.arange(nc)) % nc
    both = jnp.take(jnp.take(both, order_c, axis=0), order_z, axis=1)
    pixels = both.transpose(2, 1, 0, 3, 4).reshape(tile_rows, width, pixel_width)

    row_table = sincos_halves(row * tile_rows + jnp.arange(tile_rows, dtype=jnp.int32), model)
    col_table = sincos_halves(jnp.arange(width, dtype=jnp.int32), model)
    normed = embed_norm(
        pixels,
        w_patch,
        patch_bias.astype(jnp.float32)[None, :],
        ln_gain.astype(jnp.float32)[None, :],
        row_table,
        col_table,
    )
    weight = w_qkv.transpose(1, 2, 0, 3)
    keys = project(normed, weight, 1, qk_gain[1], "project_k")
    values = project(normed, weight, 2, None, "project_v")
    queries = project(normed, weight, 0, qk_gain[0], "project_q")

    flip = swap(nx, 1)
    keys_x = lax.ppermute(keys, "x", flip)
    keys_y = [lax.ppermute(keys, "y", swap(ny, s)) for s in range(1, ny)]
    values_x = lax.ppermute(values, "x", flip)
    values_y = [lax.ppermute(values, "y", swap(ny, s)) for s in range(1, ny)]
    keys_far = [lax.ppermute(keys_x, "y", swap(ny, s)) for s in range(1, ny)]
    values_far = [lax.ppermute(v, "x", flip) for v in values_y]

    runs = nz * nc
    state = attend(queries, [(keys, values)], None, runs, None, 1, False, "attend_own")
    near = [(keys_x, values_x)] + list(zip(keys_y, values_y))
    state = attend(queries, near, state, runs, None, 1, False, "attend_near")
    far = list(zip(keys_far, values_far))
    parts = 2
    outs = []
    for part in range(parts):
        context = attend(queries, far, state, runs, part, parts, True, "attend_far")
        partial = jnp.dot(context, out_weight, preferred_element_type=jnp.float32).astype(jnp.bfloat16)
        outs.append(lax.psum_scatter(partial, ("z", "c"), scatter_dimension=0, tiled=True))
    return jnp.concatenate(outs, axis=0)


def solution(mesh):
    rows, cols = mesh.shape["row"], mesh.shape["col"]
    fine = Mesh(mesh.devices.reshape(rows // 2, 2, cols // 2, 2), ("y", "x", "z", "c"))
    row, col = ("y", "x"), ("z", "c")
    return jax.shard_map(
        local,
        mesh=fine,
        in_specs=(
            P(row, col, None),
            P(),
            P(),
            P(),
            P(None, None, col, None),
            P(None, col, None),
            P(col, None, row),
        ),
        out_specs=P((*row, *col), None),
        check_vma=False,
    )
```

time: 634 us -> 386 us (0.61)
  matrix products: 177 us -> 17.7 us
  Pallas kernels: 0 us -> 132 us
  other arithmetic: 104 us -> 9.43 us
  waiting for transfers between devices: 248 us -> 177 us
  local copies, waits for them, and re-layouts: 88.6 us -> 22 us
  starting transfers between devices: 0.16 us -> 13.4 us
    dot_general x10 -> x0, matrix products: 162 us -> none  [the longest x4 55.5 us: step_block(): jnp.einsum('hqk,khd->hqd', exponent.astype(jnp.bfloat16), block_values, p...]
    pallas_call x0 -> x8, Pallas kernels: none -> 132 us  [the longest x4 67.5 us: attend(): pl.pallas_call(functools.partial(attend_body, pairs=len(kvs), first=state...]
    all_gather x4 -> x1, waiting for transfers between devices: 117 us -> 0.01 us  [local(): lax.all_gather(w_out, ('y', 'x'), axis=2, tiled=True)]
    ppermute x0 -> x10, waiting for transfers between devices: none -> 58.7 us  [the longest x1 43.1 us: local(): keys_x = lax.ppermute(keys, 'x', flip)]
    reduce_sum x7 -> x0, other arithmetic: 54 us -> none  [the longest x4 42.2 us: step_block(): new_total = run_total * rescale + jnp.sum(exponent, axis=2)]
    unnamed x10 -> x26, local copies, waits for them, and re-layouts: 62.5 us -> 18.1 us
    sin x1 -> x2, other arithmetic: 46.9 us -> 3.04 us  [sincos_halves(): return jnp.concatenate([jnp.sin(angle), jnp.cos(angle)], axis=1)]
    reshape x2 -> x0, local copies, waits for them, and re-layouts: 22.7 us -> none  [the longest x1 11.4 us: local(): value_piece.reshape(block_count, key_block, heads_here, head_size)]
  transfers between devices with their start and end apart: 5 -> 13, of which waited for: 3 -> 6; matrix products, arithmetic and copies ran while one was open for 44% -> 5% of each run, Pallas kernels for 0% -> 34%
where the time goes in v1:
time: 386 us; the launch traced here: 385 us
  waiting for transfers between devices  177 us (46%)
  Pallas kernels  132 us (34%)
  local copies, waits for them, and re-layouts  22 us (6%)
  matrix products  17.7 us (5%)
  starting transfers between devices  13.4 us (3%)
  between operations  13.4 us (3%)
  other arithmetic  9.43 us (2%)
    reduce_scatter x2, waiting for transfers between devices, local(): lax.psum_scatter(partial, ('z', 'c'), scatter_dimension=0, tiled=True)  118 us
    pallas_call x4, Pallas kernels, attend(): pl.pallas_call(functools.partial(attend_body, pairs=len(kvs), first=state...  67.5 us
    ppermute x1, waiting for transfers between devices, local(): keys_x = lax.ppermute(keys, 'x', flip)  43.1 us
    pallas_call x3, Pallas kernels, project(): pl.pallas_call(functools.partial(project_body, norm=norm, tile=math.gcd(t...  42.5 us
    pallas_call x1, Pallas kernels, embed_norm(): pl.pallas_call(embed_body, grid=(rows // block,), in_specs=[pl.BlockSpec(...  21.9 us
    unnamed x26, local copies, waits for them, and re-layouts  18.1 us
    dot_general x2, matrix products, local(): jnp.dot(context, out_weight, preferred_element_type=jnp.float32)  17.7 us
    ppermute x3, waiting for transfers between devices, local(): lax.ppermute(patches, 'z', swap(nz, s))  11 us
  transfers between devices with their start and end apart: 13, of which 6 were waited for; matrix products, arithmetic and copies ran while one was open for 5% of the time, Pallas kernels for 34%

profile of v1, /device:TPU:0, one launch (start us, length us, event | category | flops | bytes accessed | tf_op | source)
XLA Modules:
  0.0 385.2 jit_solution(7502976825629803341)
XLA Ops:
  7.5 3.1 collective-permute-start
  10.5 2.6 collective-permute-start.1
  15.0 3.4 collective-permute-done
  18.4 7.6 %collective-permute-done.1 = bf16[8,16,768]{2,1,0:T(8,128)(2,1)S(1)} collective-permute-done((bf16[8,16,768]{2,1,0:T(8,128)(2,1)S(1)}, bf16[8,16,768]{2,1,0:T(8,128)(2,1)S(1)}, u32[]{:S(2)}, u32[]{:S(2)}) %collective-permute-start.1) | collective-permute-done | bytes 196640 | tf_op jit(solution)/shard_map/ppermute | solution.py:239
  26.2 2.8 multiply_sine_fusion
  36.3 3.7 copy-done.3
  40.0 21.9 %embed_norm.1.x_ref = bf16[1024,6144]{1,0:T(8,128)(2,1)} custom-call(bf16[8,128,768]{2,1,0:T(8,128)(2,1)S(1)} %bitcast.33, bf16[768,6144]{1,0:T(8,128)(2,1)S(1)} %copy-done.3, f32[1,6144]{1,0:T(1,128)S(1)} %bitcast.34, f32[1,6144]{1,0:T(1,128)S(1)} %bitcast.35, f32[8,1,3072]{2,1,0:T(1,128)S(1)} %broadcast_in_dim.42.row_ref, ...), custom_call_target="tpu_custom_call" | custom-call | tf_op jit(solution)/shard_map/embed_norm/pallas_call | solution.py:63
  61.9 4.6 %copy-done = bf16[1024,6144]{1,0:T(8,128)(2,1)S(1)} copy-done((bf16[1024,6144]{1,0:T(8,128)(2,1)S(1)}, bf16[1024,6144]{1,0:T(8,128)(2,1)}, u32[]{:S(2)}) %copy-start) | copy-done | bytes 12582936
  66.5 14.6 %project_k.1.refs_1_ = bf16[6,1024,128]{2,1,0:T(8,128)(2,1)S(1)} custom-call(bf16[1024,6144]{1,0:T(8,128)(2,1)S(1)} %copy-done, bf16[3,6,6144,128]{3,2,1,0:T(8,128)(2,1)} %bitcast.36, f32[6,1,128]{2,1,0:T(1,128)S(1)} %get-tuple-element.19.refs_0_), custom_call_target="tpu_custom_call" | custom-call | tf_op jit(solution)/shard_map/project_k/pallas_call | solution.py:115
  82.6 13.3 %project_v.1.refs_2_ = bf16[6,1024,128]{2,1,0:T(8,128)(2,1)S(1)} custom-call(bf16[1024,6144]{1,0:T(8,128)(2,1)S(1)} %copy-done, bf16[3,6,6144,128]{3,2,1,0:T(8,128)(2,1)} %bitcast.37), custom_call_target="tpu_custom_call" | custom-call | tf_op jit(solution)/shard_map/project_v/pallas_call | solution.py:115
  98.5 43.1 %collective-permute-done.4.refs_1_ = bf16[6,1024,128]{2,1,0:T(8,128)(2,1)S(1)} collective-permute-done((bf16[6,1024,128]{2,1,0:T(8,128)(2,1)S(1)}, bf16[6,1024,128]{2,1,0:T(8,128)(2,1)S(1)}, u32[]{:S(2)}, u32[]{:S(2)}) %collective-permute-start.4) | collective-permute-done | bytes 1572896 | tf_op jit(solution)/shard_map/ppermute | solution.py:263
  143.7 14.6 %project_q.1.refs_0_ = bf16[6,1024,128]{2,1,0:T(8,128)(2,1)S(1)} custom-call(bf16[1024,6144]{1,0:T(8,128)(2,1)S(1)} %copy-done, bf16[3,6,6144,128]{3,2,1,0:T(8,128)(2,1)} %bitcast.38, f32[6,1,128]{2,1,0:T(1,128)S(1)} %get-tuple-element.20.refs_0_), custom_call_target="tpu_custom_call" | custom-call | tf_op jit(solution)/shard_map/project_q/pallas_call | solution.py:115
  158.4 15.8 %attend_own.1 = (f32[6,1024,128]{2,1,0:T(8,128)S(1)}, f32[6,1024,256]{2,1,0:T(8,128)S(1)}) custom-call(bf16[6,1024,128]{2,1,0:T(8,128)(2,1)S(1)} %project_q.1.refs_0_, bf16[6,1024,128]{2,1,0:T(8,128)(2,1)S(1)} %project_k.1.refs_1_, bf16[6,1024,128]{2,1,0:T(8,128)(2,1)S(1)} %project_v.1.refs_2_), custom_call_target="tpu_custom_call" | custom-call | tf_op jit(solution)/shard_map/attend_own/pallas_call | solution.py:211
  174.1 2.6 copy-done.6
  176.8 27.6 %attend_near.1 = (f32[6,1024,128]{2,1,0:T(8,128)S(1)}, f32[6,1024,256]{2,1,0:T(8,128)}) custom-call(bf16[6,1024,128]{2,1,0:T(8,128)(2,1)S(1)} %project_q.1.refs_0_, bf16[6,1024,128]{2,1,0:T(8,128)(2,1)S(1)} %collective-permute-done.4.refs_1_, bf16[6,1024,128]{2,1,0:T(8,128)(2,1)} %collective-permute-done.8.refs_2_, ...), custom_call_target="tpu_custom_call" | custom-call | tf_op jit(solution)/shard_map/attend_near/pallas_call | solution.py:211
  204.4 4.6 %collective-permute-done.5.refs_1_ = bf16[6,1024,128]{2,1,0:T(8,128)(2,1)S(1)} collective-permute-done((bf16[6,1024,128]{2,1,0:T(8,128)(2,1)S(1)}, bf16[6,1024,128]{2,1,0:T(8,128)(2,1)S(1)}, u32[]{:S(2)}, u32[]{:S(2)}) %collective-permute-start.5) | collective-permute-done | bytes 1572896 | tf_op jit(solution)/shard_map/ppermute | solution.py:267
  209.0 12.0 %attend_far.2 = bf16[512,768]{1,0:T(8,128)(2,1)S(1)} custom-call(bf16[6,8,2,64,128]{4,3,2,1,0:T(8,128)(2,1)S(1)} %bitcast.29, bf16[6,1024,128]{2,1,0:T(8,128)(2,1)S(1)} %collective-permute-done.5.refs_1_, bf16[6,1024,128]{2,1,0:T(8,128)(2,1)S(1)} %collective-permute-done.7.refs_2_, f32[6,8,2,64,128]{4,3,2,1,0:T(8,128)S(1)} %bitcast.31, ...), custom_call_target="tpu_custom_call" | custom-call | tf_op jit(solution)/shard_map/attend_far/pallas_call | solution.py:211
  224.8 10.8 %convolution_convert_fusion.1 = bf16[512,6144]{1,0:T(8,128)(2,1)} fusion(bf16[512,768]{1,0:T(8,128)(2,1)} %copy-done.7, bf16[768,6144]{1,0:T(8,128)(2,1)} %bitcast.46), kind=kOutput, calls=%fused_computation.3 | convolution fusion | flops 4834983936 | bytes 16515072 | tf_op jit(solution)/shard_map/dot_general | solution.py:279
  235.6 1.9 copy-done.2
  238.9 12.1 %attend_far.3 = bf16[512,768]{1,0:T(8,128)(2,1)S(1)} custom-call(bf16[6,8,2,64,128]{4,3,2,1,0:T(8,128)(2,1)S(1)} %bitcast.30, bf16[6,1024,128]{2,1,0:T(8,128)(2,1)S(1)} %collective-permute-done.5.refs_1_, bf16[6,1024,128]{2,1,0:T(8,128)(2,1)S(1)} %copy-done.5, f32[6,8,2,64,128]{4,3,2,1,0:T(8,128)S(1)} %bitcast.32, f32[6,8,2,64,256]{4,3,2,1,0:T(8,128)} %bitcast.40), custom_call_target="tpu_custom_call" | custom-call | tf_op jit(solution)/shard_map/attend_far/pallas_call | solution.py:211
  251.1 6.9 %convolution_convert_fusion = bf16[512,6144]{1,0:T(8,128)(2,1)} fusion(bf16[512,768]{1,0:T(8,128)(2,1)S(1)} %attend_far.3, bf16[768,6144]{1,0:T(8,128)(2,1)S(1)} %bitcast.47), kind=kOutput, calls=%fused_computation.2 | convolution fusion | flops 4834983936 | bytes 16515072 | tf_op jit(solution)/shard_map/dot_general | solution.py:279
  258.0 47.5 %reduce-scatter.3.cloned.1.call-done = bf16[64,6144]{1,0:T(8,128)(2,1)} async-done(((bf16[512,6144]{1,0:T(8,128)(2,1)}), bf16[64,6144]{1,0:T(8,128)(2,1)}) %reduce-scatter.3.cloned.1.call-update) | async-done | bytes 786448 | tf_op jit(solution)/shard_map/reduce_scatter | solution.py:280
  305.5 70.5 %reduce-scatter.5.cloned.1.call-done = bf16[64,6144]{1,0:T(8,128)(2,1)} async-done(((bf16[512,6144]{1,0:T(8,128)(2,1)}), bf16[64,6144]{1,0:T(8,128)(2,1)}) %reduce-scatter.5.cloned.1.call-update) | async-done | bytes 786448 | tf_op jit(solution)/shard_map/reduce_scatter | solution.py:280
  376.0 2.7 pad_maximum_fusion.2
  (66 shorter events, 21.7 us)
Async XLA Ops:
  6.5 8.3 %copy-start.9 = (bf16[6144]{0:T(1024)(128)(2,1)S(1)}, bf16[6144]{0:T(1024)(128)(2,1)}, u32[]{:S(2)}) copy-start(bf16[6144]{0:T(1024)(128)(2,1)} %param.9) | copy-start | bytes 36868
  6.5 8.3 %copy-start.10 = (bf16[6144]{0:T(1024)(128)(2,1)S(1)}, bf16[6144]{0:T(1024)(128)(2,1)}, u32[]{:S(2)}) copy-start(bf16[6144]{0:T(1024)(128)(2,1)} %param.10) | copy-start | bytes 36868
  6.5 8.4 %copy-start.11 = (f32[2,6,128]{2,0,1:T(2,128)S(1)}, f32[2,6,128]{2,0,1:T(2,128)}, u32[]{:S(2)}) copy-start(f32[2,6,128]{2,0,1:T(2,128)} %param.12) | copy-start | bytes 18436
  6.5 218.2 %all-gather.2.cloned.1.call-start = ((), (), s32[]{:S(2)}) async-start(), calls=%async_computation.2 | async-start | bytes 11796480 | tf_op jit(solution)/shard_map/all_gather | solution.py:237
  7.3 298.2 %reduce-scatter.3.cloned.1.call-start = ((), (), s32[]{:S(2)}) async-start(), calls=%async_computation.3 | async-start | bytes 7077888 | tf_op jit(solution)/shard_map/reduce_scatter | solution.py:280
  7.5 11.0 %collective-permute-start = (bf16[8,16,768]{2,1,0:T(8,128)(2,1)S(1)}, bf16[8,16,768]{2,1,0:T(8,128)(2,1)S(1)}, u32[]{:S(2)}, u32[]{:S(2)}) collective-permute-start(bf16[8,16,768]{2,1,0:T(8,128)(2,1)S(1)} %copy-done.8), channel_id=1, source_target_pairs={{0,2},{2,4},{4,6},{6,0},{1,3},{3,5},{5,7},{7,1},{8,10},{10,12},{12... | collective-permute-start | bytes 589832 | tf_op jit(solution)/shard_map/ppermute | solution.py:239
  10.5 15.5 %collective-permute-start.1 = (bf16[8,16,768]{2,1,0:T(8,128)(2,1)S(1)}, bf16[8,16,768]{2,1,0:T(8,128)(2,1)S(1)}, u32[]{:S(2)}, u32[]{:S(2)}) collective-permute-start(bf16[8,16,768]{2,1,0:T(8,128)(2,1)S(1)} %copy-done.8), channel_id=1, source_target_pairs={{0,4},{2,6},{4,0},{6,2},{1,5},{3,7},{5,1},{7,3},{8,12},{10,14},{12... | collective-permute-start | bytes 589832 | tf_op jit(solution)/shard_map/ppermute | solution.py:239
  13.1 12.9 %collective-permute-start.2 = (bf16[8,16,768]{2,1,0:T(8,128)(2,1)S(1)}, bf16[8,16,768]{2,1,0:T(8,128)(2,1)S(1)}, u32[]{:S(2)}, u32[]{:S(2)}) collective-permute-start(bf16[8,16,768]{2,1,0:T(8,128)(2,1)S(1)} %copy-done.8), channel_id=1, source_target_pairs={{0,6},{2,0},{4,2},{6,4},{1,7},{3,1},{5,3},{7,5},{8,14},{10,8},{12,... | collective-permute-start | bytes 589832 | tf_op jit(solution)/shard_map/ppermute | solution.py:239
  26.1 3.0 collective-permute-start.3
  36.3 3.7 copy-start.3
  61.9 4.6 %copy-start = (bf16[1024,6144]{1,0:T(8,128)(2,1)S(1)}, bf16[1024,6144]{1,0:T(8,128)(2,1)}, u32[]{:S(2)}) copy-start(bf16[1024,6144]{1,0:T(8,128)(2,1)} %embed_norm.1.x_ref) | copy-start | bytes 37748740
  81.1 60.6 %collective-permute-start.4 = (bf16[6,1024,128]{2,1,0:T(8,128)(2,1)S(1)}, bf16[6,1024,128]{2,1,0:T(8,128)(2,1)S(1)}, u32[]{:S(2)}, u32[]{:S(2)}) collective-permute-start(bf16[6,1024,128]{2,1,0:T(8,128)(2,1)S(1)} %project_k.1.refs_1_), channel_id=1, source_target_pairs={{0,8},{8,0},{1,9},{9,1},{2,10},{10,2},{3,11},{11,3},{4,12},{12,4},... | collective-permute-start | bytes 4718600 | tf_op jit(solution)/shard_map/ppermute | solution.py:263
  95.9 47.3 %collective-permute-start.6 = (bf16[6,1024,128]{2,1,0:T(8,128)(2,1)S(1)}, bf16[6,1024,128]{2,1,0:T(8,128)(2,1)}, u32[]{:S(2)}, u32[]{:S(2)}) collective-permute-start(bf16[6,1024,128]{2,1,0:T(8,128)(2,1)S(1)} %project_v.1.refs_2_), channel_id=1, source_target_pairs={{0,16},{16,0},{1,17},{17,1},{2,18},{18,2},{3,19},{19,3},{4,20},{20... | collective-permute-start | bytes 4718600 | tf_op jit(solution)/shard_map/ppermute | solution.py:266
  97.5 79.3 %collective-permute-start.9 = (bf16[6,1024,128]{2,1,0:T(8,128)(2,1)S(1)}, bf16[6,1024,128]{2,1,0:T(8,128)(2,1)}, u32[]{:S(2)}, u32[]{:S(2)}) collective-permute-start(bf16[6,1024,128]{2,1,0:T(8,128)(2,1)S(1)} %project_k.1.refs_1_), channel_id=1, source_target_pairs={{0,16},{16,0},{1,17},{17,1},{2,18},{18,2},{3,19},{19,3},{4,20},{20... | collective-permute-start | bytes 4718600 | tf_op jit(solution)/shard_map/ppermute | solution.py:264
  98.0 78.8 %collective-permute-start.8 = (bf16[6,1024,128]{2,1,0:T(8,128)(2,1)S(1)}, bf16[6,1024,128]{2,1,0:T(8,128)(2,1)}, u32[]{:S(2)}, u32[]{:S(2)}) collective-permute-start(bf16[6,1024,128]{2,1,0:T(8,128)(2,1)S(1)} %project_v.1.refs_2_), channel_id=1, source_target_pairs={{0,8},{8,0},{1,9},{9,1},{2,10},{10,2},{3,11},{11,3},{4,12},{12,4},... | collective-permute-start | bytes 4718600 | tf_op jit(solution)/shard_map/ppermute | solution.py:265
  141.7 67.3 %collective-permute-start.5 = (bf16[6,1024,128]{2,1,0:T(8,128)(2,1)S(1)}, bf16[6,1024,128]{2,1,0:T(8,128)(2,1)S(1)}, u32[]{:S(2)}, u32[]{:S(2)}) collective-permute-start(bf16[6,1024,128]{2,1,0:T(8,128)(2,1)S(1)} %collective-permute-done.4.refs_1_), channel_id=1, source_target_pairs={{0,16},{16,0},{1,17},{17,1},{2,18},{18,2},{3,19},{19,3},{4,20},{20... | collective-permute-start | bytes 4718600 | tf_op jit(solution)/shard_map/ppermute | solution.py:267
  143.2 65.8 %collective-permute-start.7 = (bf16[6,1024,128]{2,1,0:T(8,128)(2,1)}, bf16[6,1024,128]{2,1,0:T(8,128)(2,1)S(1)}, u32[]{:S(2)}, u32[]{:S(2)}) collective-permute-start(bf16[6,1024,128]{2,1,0:T(8,128)(2,1)} %collective-permute-done.6.refs_4_), channel_id=1, source_target_pairs={{0,8},{8,0},{1,9},{9,1},{2,10},{10,2},{3,11},{11,3},{4,12},{12,4},... | collective-permute-start | bytes 4718600 | tf_op jit(solution)/shard_map/ppermute | solution.py:268
  174.1 2.6 copy-start.6
  221.0 1.7 copy-start.1
  222.7 1.1 copy-start.4
  235.6 140.4 %reduce-scatter.5.cloned.1.call-start = ((), (), s32[]{:S(2)}) async-start(), calls=%async_computation.4 | async-start | bytes 7077888 | tf_op jit(solution)/shard_map/reduce_scatter | solution.py:280
  235.6 1.9 copy-start.2
  237.5 1.4 copy-start.5
  238.9 12.1 %copy-start.12 = (bf16[6,128,6144]{2,1,0:T(8,128)(2,1)S(1)}, bf16[6,128,6144]{2,1,0:T(8,128)(2,1)}, u32[]{:S(2)}) copy-start(bf16[6,128,6144]{2,1,0:T(8,128)(2,1)} %all-gather.2.cloned.1.call-done) | copy-start | bytes 28311556
  (2 other events, 1.9 us)
Sparse Core Ops, SparseCore 0:
  9.2 122.6 all-gather.1
  235.7 69.7 reduce-scatter.2
  307.8 68.1 reduce-scatter.4
